TPU v7x, 32 devices: a whole 2x2x4 slice. The times are simulated.
32 devices in a mesh: row: 4 (over y, core), col: 8 (over z, x).
Axes of the slice: x: 2, y: 2, z: 4, core: 2. Of those that a mesh axis runs over, the one named last changes fastest.
Arguments:
- out_weights: bfloat16 [2048, 2048], P('row', 'col'), may hold values from -1 to 1
- in_weights: bfloat16 [2048, 2048], P('row', 'col'), may hold values from -1 to 1, as said below
- tile_list: int32 [16, 12], replicated, may hold values from 0 to 15, as said below
- tile_count: int32 [16], replicated, may hold values from 1 to 12, as said below
- owner: int32 [16], replicated, may hold values from 0 to 3, as said below
Outputs:
- transitive: float32 [2048], P('row')
- cyclic: float32 [2048], P('row')
Inputs may be any that keep to these rules, and one draw needn't show every extreme that they name: in_weights is the transpose of out_weights. `tile_list`: the 12 entries of a row are distinct tile columns. Only the first tile_count[a] entries of row a of tile_list are live. `owner`: each index of row owns exactly 4 tile rows, and at most 1 of the tile rows s * 4 to (s + 1) * 4 - 1, for every s; tile row t is owned by the index (t // 4 + e) mod 4 for some e from 0 to 3.
All inputs are finite; a program needn't handle non-finite values.
Results may differ from a plain program's by a relative error of at most 0.0003.
Values may be sent and summed in bfloat16 or wider, within the bound.
A program may use at most 64 MiB of HBM per device.

v0:
```python
import jax
import jax.numpy as jnp
from jax import lax
from jax.sharding import PartitionSpec as P

TILE = 128


def from_behind(x, axis, by):
    length = lax.axis_size(axis)
    return lax.ppermute(x, axis, [(i, (i + by) % length) for i in range(length)])


def tile_mask(tile_list, tile_count):
    tile_total = tile_list.shape[0]
    live_slots = jnp.arange(tile_list.shape[1], dtype=jnp.int32)[None, :] < tile_count[:, None]
    matches = (
        tile_list[:, :, None] == jnp.arange(tile_total, dtype=jnp.int32)[None, None, :]
    ) & live_slots[:, :, None]
    return jnp.any(matches, axis=1)


def block_of(full_mask, row_start, col_start, tile_rows, tile_cols):
    window = lax.dynamic_slice(full_mask, (row_start, col_start), (tile_rows, tile_cols))
    return jnp.repeat(jnp.repeat(window, TILE, axis=0), TILE, axis=1)


def to_owners(in_block, owner, owned_tiles, my_row, row_count, tile_rows, pair_slots):
    cols_blk = in_block.shape[1]
    tile_stack = in_block.reshape(tile_rows, TILE, cols_blk)
    owner_grid = owner.reshape(row_count, tile_rows)
    targets = lax.dynamic_index_in_dim(owner_grid, my_row, 0, keepdims=False)
    distance = (targets - my_row + row_count) % row_count
    position = jnp.arange(tile_rows, dtype=jnp.int32)
    earlier = (targets[:, None] == targets[None, :]) & (position[None, :] < position[:, None])
    slot_of = jnp.sum(earlier, axis=1)
    slot_ids = jnp.arange(pair_slots, dtype=jnp.int32)
    reach = min(tile_rows, row_count)
    arrivals = []
    for offset in range(reach):
        chosen = (distance[None, :] == offset) & (slot_of[None, :] == slot_ids[:, None])
        picked = jnp.sum(jnp.where(chosen, position[None, :], 0), axis=1)
        filled = jnp.any(chosen, axis=1)
        outgoing = jnp.where(
            filled[:, None, None],
            jnp.take(tile_stack, picked, axis=0),
            jnp.zeros((), in_block.dtype),
        )
        if offset == 0:
            arrivals.append(outgoing)
        else:
            arrivals.append(from_behind(outgoing, "row", offset))
    arrived = jnp.stack(arrivals, axis=0).reshape(reach * pair_slots, TILE, cols_blk)
    source_row = owned_tiles // tile_rows
    within = owned_tiles % tile_rows
    peer_owners = jnp.take(owner_grid, source_row, axis=0)
    slot_in = jnp.sum((peer_owners == my_row) & (position[None, :] < within[:, None]), axis=1)
    from_distance = (my_row - source_row + row_count) % row_count
    arrival_index = from_distance * pair_slots + slot_in
    return jnp.take(arrived, arrival_index, axis=0).reshape(tile_rows * TILE, cols_blk)


def per_device(out_weights, in_weights, tile_list, tile_count, owner):
    rows_blk, cols_blk = out_weights.shape
    tile_rows = rows_blk // TILE
    tile_cols = cols_blk // TILE
    row_count = lax.axis_size("row")
    pair_slots = max(1, tile_rows // row_count)
    my_row = lax.axis_index("row")
    my_col = lax.axis_index("col")
    listed = tile_mask(tile_list, tile_count)
    out_keep = block_of(listed, my_row * tile_rows, my_col * tile_cols, tile_rows, tile_cols)
    in_keep = block_of(listed.T, my_row * tile_rows, my_col * tile_cols, tile_rows, tile_cols)
    zero_value = jnp.zeros((), out_weights.dtype)
    out_block = jnp.where(out_keep, out_weights, zero_value)
    in_block = jnp.where(in_keep, in_weights, zero_value)
    owner_order = jnp.argsort(owner, stable=True)
    owned_tiles = lax.dynamic_slice_in_dim(owner_order, my_row * tile_rows, tile_rows, 0)
    owned_nodes = (
        owned_tiles[:, None] * TILE + jnp.arange(TILE, dtype=jnp.int32)[None, :]
    ).reshape(-1)
    out_panel = lax.all_gather(out_block, "row", axis=0, tiled=True)
    in_owned = to_owners(in_block, owner, owned_tiles, my_row, row_count, tile_rows, pair_slots)
    out_owned = jnp.take(out_panel, owned_nodes, axis=0)
    two_paths = jnp.dot(
        lax.all_gather(out_owned, "col", axis=1, tiled=True),
        out_panel,
        preferred_element_type=jnp.float32,
    )
    transitive_part = jnp.sum(out_owned.astype(jnp.float32) * two_paths, axis=1)
    cyclic_part = jnp.sum(in_owned.astype(jnp.float32) * two_paths, axis=1)
    transitive, cyclic = lax.psum((transitive_part, cyclic_part), "col")
    return (transitive, cyclic)


def solution(mesh):
    in_specs = (P("row", "col"), P("row", "col"), P(), P(), P())
    out_specs = (P("row"), P("row"))
    return jax.shard_map(
        per_device, mesh=mesh, in_specs=in_specs, out_specs=out_specs, check_vma=False
    )
```

profile of v0, /device:TPU:0, one launch (start us, length us, event | category | flops | bytes accessed | tf_op | source)
XLA Modules:
  0.0 112.7 jit_solution(10930796440918249726)
XLA Ops:
  7.2 0.0 all-gather.3.cloned.1.call-start
  7.2 0.8 copy.17
  8.0 0.7 iota_compare_fusion.1
  8.7 0.1 fusion.1
  8.8 0.1 dynamic_slice.14
  8.9 0.1 copy.18
  9.0 0.1 broadcast_bitcast_fusion.1
  9.1 0.3 copy.19
  9.4 1.7 %broadcast_select_fusion.2 = bf16[512,256]{1,0:T(8,128)(2,1)} fusion(pred[512,256]{1,0:T(8,128)(4,1)S(1)} %copy.19, bf16[512,256]{1,0:T(8,128)(2,1)} %param.7), kind=kLoop, calls=%fused_computation.8 | loop fusion | flops 131072 | bytes 655360 | tf_op jit(solution)/shard_map/jit(_where)/select_n | solution.py:75
  11.1 0.0 all-gather.3.cloned.1.call-update
  11.1 0.0 copy-start.1
  11.1 0.0 all-gather.5.cloned.1.call-start
  11.2 1.9 %sort.17 = (s32[16]{0:T(128)}, s32[16]{0:T(128)S(1)}) sort(s32[16]{0:T(128)} %param.11, s32[16]{0:T(128)S(1)} %iota.34), dimensions={0}, to_apply=%region_0.0 | sort | flops 64 | bytes 256 | tf_op jit(solution)/shard_map/jit(argsort)/sort | solution.py:77
  13.1 0.1 broadcast_multiply_fusion
  13.2 0.1 iota_add_fusion
  13.2 0.1 compare_and_fusion.2
  13.3 17.3 %all-gather.3.cloned.1.call-done = bf16[2048,256]{1,0:T(8,128)(2,1)} async-done(((bf16[512,256]{1,0:T(8,128)(2,1)}), bf16[2048,256]{1,0:T(8,128)(2,1)}) %all-gather.3.cloned.1.call-update) | async-done | bytes 1048592 | tf_op jit(solution)/shard_map/all_gather | solution.py:82
  30.7 2.9 %gather_fusion = bf16[512,256]{1,0:T(8,128)(2,1)S(1)} fusion(bf16[2048,256]{1,0:T(8,128)(2,1)} %all-gather.3.cloned.1.call-done, s32[1024]{0:T(1024)S(1)} %pad_clamp_fusion.2), kind=kCustom, calls=%fused_computation | custom fusion | bytes 526336 | tf_op jit(solution)/shard_map/jit(_take)/gather | solution.py:84
  33.6 0.1 copy.20
  33.7 0.0 copy-start
  33.7 0.7 broadcast_select_fusion
  34.5 0.0 all-gather.5.cloned.1.call-update
  34.5 0.0 copy-done.2
  34.5 0.1 reshape.174
  34.6 0.2 convert_reduce_fusion
  34.8 0.8 fusion.9
  35.6 0.7 select_reduce_fusion.3
  43.9 0.1 dynamic-slice_bitcast_fusion
  44.0 0.1 broadcast_bitcast_fusion
  44.1 0.3 copy.21
  44.4 0.0 copy-done.1
  44.5 2.6 %fusion.2 = (bf16[1,1,128,256]{3,2,0,1:T(8,128)(2,1)S(1)}, bf16[1,128,256]{2,1,0:T(8,128)(2,1)S(1)}, bf16[1,128,256]{2,1,0:T(8,128)(2,1)S(1)}, bf16[1,128,256]{2,1,0:T(8,128)(2,1)S(1)}) fusion(bf16[4,128,256]{2,1,0:T(8,128)(2,1)S(1)} %bitcast.79, s32[]{:T(128)} %bitcast.12, pred[]{:T(512)} %bitcast.8, pred[]{:T(512)} %get-tuple-element.18, s32[]{:T(128)} %bitcast.27, ...), kind=kLoop, calls=%fused_computation.16 | loop fusion | flops 262144 | bytes 524312 | tf_op jit(solution)/shard_map/stack | solution.py:53
  47.0 0.2 collective-permute-start.2
  47.3 1.7 %collective-permute-start.1 = (bf16[1,128,256]{2,1,0:T(8,128)(2,1)S(1)}, bf16[1,128,256]{2,1,0:T(8,128)(2,1)S(1)}, u32[]{:S(2)}, u32[]{:S(2)}) collective-permute-start(bf16[1,128,256]{2,1,0:T(8,128)(2,1)S(1)} %get-tuple-element.36), channel_id=1, source_target_pairs={{0,16},{8,24},{16,0},{24,8},{1,17},{9,25},{17,1},{25,9},{2,18},{10... | collective-permute-start | bytes 196616 | tf_op jit(solution)/shard_map/ppermute | solution.py:11
  48.9 0.0 collective-permute-start
  48.9 0.1 compare_and_fusion.1
  49.1 0.6 gather_fusion.1
  49.6 0.2 convert_reduce_fusion.1
  49.8 0.1 broadcast_bitcast_fusion.2
  49.9 0.0 collective-permute-done.2
  49.9 2.7 %collective-permute-done.1 = bf16[1,128,256]{2,1,0:T(8,128)(2,1)S(1)} collective-permute-done((bf16[1,128,256]{2,1,0:T(8,128)(2,1)S(1)}, bf16[1,128,256]{2,1,0:T(8,128)(2,1)S(1)}, u32[]{:S(2)}, u32[]{:S(2)}) %collective-permute-start.1) | collective-permute-done | bytes 65568 | tf_op jit(solution)/shard_map/ppermute | solution.py:11
  52.7 0.3 collective-permute-done
  53.0 0.6 gather_fusion.2
  53.6 0.1 copy.26
  53.8 30.0 %all-gather.5.cloned.1.call-done = bf16[512,2048]{0,1:T(8,128)(2,1)} async-done(((bf16[512,256]{0,1:T(8,128)(2,1)}), bf16[512,2048]{0,1:T(8,128)(2,1)}) %all-gather.5.cloned.1.call-update) | async-done | bytes 2097168 | tf_op jit(solution)/shard_map/all_gather | solution.py:86
  83.8 2.3 %fusion.13 = f32[512,256]{0,1:T(8,128)S(1)} fusion(bf16[512,2048]{0,1:T(8,128)(2,1)} %all-gather.5.cloned.1.call-done, bf16[2048,256]{1,0:T(8,128)(2,1)S(1)} %copy-done), kind=kOutput, calls=%fused_computation.72 | convolution fusion | flops 536870912 | bytes 3670016 | tf_op jit(solution)/shard_map/dot_general | solution.py:85
  86.1 0.2 multiply_reduce_fusion
  86.3 19.5 %all-reduce = (f32[512]{0:T(512)}, f32[512]{0:T(512)}) all-reduce(f32[512]{0:T(512)S(1)} %get-tuple-element.17, f32[512]{0:T(512)S(1)} %get-tuple-element.16), channel_id=1, replica_groups=mesh['row'=4,'col'=8] {'col'}, use_global_device_ids=true, to_apply=%region_3.4 | all-reduce | flops 1024 | bytes 8192 | tf_op jit(solution)/shard_map/psum | solution.py:92
  (16 shorter events, 0.2 us)
Async XLA Ops:
  7.2 23.5 %all-gather.3.cloned.1.call-start = ((), (), s32[]{:S(2)}) async-start(), calls=%async_computation | async-start | bytes 1310720 | tf_op jit(solution)/shard_map/all_gather | solution.py:82
  11.1 23.5 %copy-start.2 = (s32[16]{0:T(128)S(1)}, s32[16]{0:T(128)}, u32[]{:S(2)}) copy-start(s32[16]{0:T(128)} %param.11) | copy-start | bytes 196
  11.1 33.3 %copy-start.1 = (bf16[512,256]{1,0:T(8,128)(2,1)S(1)}, bf16[512,256]{1,0:T(8,128)(2,1)}, u32[]{:S(2)}) copy-start(bf16[512,256]{1,0:T(8,128)(2,1)} %param.8) | copy-start | bytes 786436
  11.1 72.7 %all-gather.5.cloned.1.call-start = ((), (), s32[]{:S(2)}) async-start(), calls=%async_computation.1 | async-start | bytes 2359296 | tf_op jit(solution)/shard_map/all_gather | solution.py:86
  33.7 50.0 %copy-start = (bf16[2048,256]{1,0:T(8,128)(2,1)S(1)}, bf16[2048,256]{1,0:T(8,128)(2,1)}, u32[]{:S(2)}) copy-start(bf16[2048,256]{1,0:T(8,128)(2,1)} %all-gather.3.cloned.1.call-done) | copy-start | bytes 3145732
  47.0 2.9 %collective-permute-start.2 = (bf16[1,128,256]{2,1,0:T(8,128)(2,1)S(1)}, bf16[1,128,256]{2,1,0:T(8,128)(2,1)S(1)}, u32[]{:S(2)}, u32[]{:S(2)}) collective-permute-start(bf16[1,128,256]{2,1,0:T(8,128)(2,1)S(1)} %get-tuple-element.35), channel_id=1, source_target_pairs={{0,24},{8,0},{16,8},{24,16},{1,25},{9,1},{17,9},{25,17},{2,26},{10... | collective-permute-start | bytes 196616 | tf_op jit(solution)/shard_map/ppermute | solution.py:11
  47.3 5.4 %collective-permute-start.1 = (bf16[1,128,256]{2,1,0:T(8,128)(2,1)S(1)}, bf16[1,128,256]{2,1,0:T(8,128)(2,1)S(1)}, u32[]{:S(2)}, u32[]{:S(2)}) collective-permute-start(bf16[1,128,256]{2,1,0:T(8,128)(2,1)S(1)} %get-tuple-element.36), channel_id=1, source_target_pairs={{0,16},{8,24},{16,0},{24,8},{1,17},{9,25},{17,1},{25,9},{2,18},{10... | collective-permute-start | bytes 196616 | tf_op jit(solution)/shard_map/ppermute | solution.py:11
  48.9 4.1 %collective-permute-start = (bf16[1,128,256]{2,1,0:T(8,128)(2,1)S(1)}, bf16[1,128,256]{2,1,0:T(8,128)(2,1)S(1)}, u32[]{:S(2)}, u32[]{:S(2)}) collective-permute-start(bf16[1,128,256]{2,1,0:T(8,128)(2,1)S(1)} %get-tuple-element.37), channel_id=1, source_target_pairs={{0,8},{8,16},{16,24},{24,0},{1,9},{9,17},{17,25},{25,1},{2,10},{10... | collective-permute-start | bytes 196616 | tf_op jit(solution)/shard_map/ppermute | solution.py:11
Sparse Core Ops, SparseCore 0:
  11.2 19.4 all-gather.2
  34.6 49.0 all-gather.4
where the time goes:
time: 113 us
  waiting for transfers between devices  50.5 us (45%)
  between operations  21.8 us (19%)
  blocking collectives  19.5 us (17%)
  other arithmetic  10.2 us (9%)
  local copies, waits for them, and re-layouts  6.35 us (6%)
  matrix products  2.35 us (2%)
  starting transfers between devices  1.99 us (2%)
    all_gather x1, waiting for transfers between devices, per_device(): lax.all_gather(out_owned, 'col', axis=1, tiled=True)  30 us
    psum x1, blocking collectives, per_device(): transitive, cyclic = lax.psum((transitive_part, cyclic_part), 'col')  19.5 us
    all_gather x1, waiting for transfers between devices, per_device(): out_panel = lax.all_gather(out_block, 'row', axis=0, tiled=True)  17.3 us
    ppermute x3, waiting for transfers between devices, from_behind(): lax.ppermute(x, axis, [(i, (i + by) % length) for i in range(length)])  3.09 us
    gather x2, local copies, waits for them, and re-layouts, per_device(): out_owned = jnp.take(out_panel, owned_nodes, axis=0)  3.06 us
    another operation x1, other arithmetic, to_owners(): jnp.stack(arrivals, axis=0).reshape(reach * pair_slots, TILE, cols_blk)  2.58 us
    dot_general x1, matrix products, per_device(): jnp.dot(lax.all_gather(out_owned, 'col', axis=1, tiled=True), out_panel,...  2.35 us
  transfers between devices with their start and end apart: 5, of which 4 were waited for; matrix products, arithmetic and copies ran while one was open for 8% of the time, Pallas kernels for 0%

commit v1 on v0

v1 whole, which is shorter than its diff:
```python
import functools

import jax
import jax.numpy as jnp
from jax import lax
from jax.experimental import pallas as pl
from jax.experimental.pallas import tpu as pltpu
from jax.sharding import PartitionSpec as P

TILE = 128
HALVES = 2
MESH = pl.DeviceIdType.MESH


def kernel(rows_n, cols_n, out_ref, in_ref, list_ref, count_ref, owner_ref, trans_ref, cyc_ref,
           own, colp, rowp, inb, mask, acc, sendbuf, recvbuf,
           load_sem, local_sem, swap_send, swap_recv, col_send, col_recv, in_send, in_recv,
           up_send, dn_send, sib_send, row_recv, res_send, res_recv):
    rb, cb = out_ref.shape
    tr, ct = rb // TILE, cb // TILE
    nt, slots = list_ref.shape
    lines = cols_n // 2
    reach = sendbuf.shape[0]
    hb = rb // HALVES
    me_r, me_c = lax.axis_index("row"), lax.axis_index("col")
    yy, p = me_r // 2, me_r % 2
    zz, a = me_c // 2, me_c % 2
    vr, vc = 2 * yy + a, 2 * zz + p

    def home(r, c):
        return (2 * (r // 2) + c % 2, 2 * (c // 2) + r % 2)

    load = pltpu.make_async_copy(out_ref, own, load_sem)
    load.start()

    barrier = pltpu.get_barrier_semaphore()

    def greet(i, carry):
        there = (me_r + i // cols_n) % rows_n, (me_c + i % cols_n) % cols_n
        pl.semaphore_signal(barrier, inc=1, device_id=there, device_id_type=MESH)
        return carry

    lax.fori_loop(1, rows_n * cols_n, greet, 0)
    load.wait()
    pl.semaphore_wait(barrier, rows_n * cols_n - 1)

    def half(h):
        return pl.ds(h * hb, hb)

    def col_at(group, h):
        return pl.ds(pl.multiple_of(group * rb + h * hb, hb), hb)

    swap = home(me_r, me_c)
    swaps = [
        pltpu.make_async_remote_copy(
            src_ref=own.at[half(h)], dst_ref=colp.at[col_at(me_r, h)], send_sem=swap_send.at[h],
            recv_sem=swap_recv.at[h], device_id=swap, device_id_type=MESH)
        for h in range(HALVES)
    ]
    swaps_here = [
        pltpu.make_async_copy(own.at[half(h)], colp.at[col_at(me_r, h)], swap_recv.at[h])
        for h in range(HALVES)
    ]
    give_in = pltpu.make_async_remote_copy(
        src_ref=in_ref, dst_ref=inb, send_sem=in_send, recv_sem=in_recv, device_id=swap, device_id_type=MESH)
    keep_in = pltpu.make_async_copy(in_ref, inb, in_recv)

    def col_copy(s):
        return pltpu.make_async_remote_copy(
            src_ref=own, dst_ref=colp.at[pl.ds(pl.multiple_of(me_r * rb, rb), rb)],
            send_sem=col_send.at[s], recv_sem=col_recv.at[s],
            device_id=home((me_r + s) % rows_n, me_c), device_id_type=MESH)

    @pl.when(a == p)
    def _():
        for h in range(HALVES):
            swaps_here[h].start()
        keep_in.start()

    @pl.when(a != p)
    def _():
        for h in range(HALVES):
            swaps[h].start()

    def up(slot, h, src):
        return pltpu.make_async_remote_copy(
            src_ref=src, dst_ref=rowp.at[slot, half(h)], send_sem=up_send.at[slot, h],
            recv_sem=row_recv.at[slot, h], device_id=(me_r, me_c + 2), device_id_type=MESH)

    def down(slot, h, src):
        return pltpu.make_async_remote_copy(
            src_ref=src, dst_ref=rowp.at[slot, half(h)], send_sem=dn_send.at[slot, h],
            recv_sem=row_recv.at[slot, h], device_id=(me_r, me_c - 2), device_id_type=MESH)

    def sib(slot, h, src):
        return pltpu.make_async_remote_copy(
            src_ref=src, dst_ref=rowp.at[slot, half(h)], send_sem=sib_send.at[slot, h],
            recv_sem=row_recv.at[slot, h], device_id=(2 * yy + 1 - p, me_c), device_id_type=MESH)

    def wait_row(slot, h):
        pltpu.make_async_copy(rowp.at[slot, half(h)], rowp.at[slot, half(h)], row_recv.at[slot, h]).wait()

    for h in range(HALVES):
        pltpu.make_async_copy(own.at[half(h)], colp.at[col_at(vr, h)], swap_recv.at[h]).wait()
        src = colp.at[col_at(vr, h)]

        @pl.when(zz < lines - 1)
        def _():
            up(vc, h, src).start()

        @pl.when(zz > 0)
        def _():
            down(vc, h, src).start()

        sib(vc, h, src).start()
        if h == 0:
            lax.fori_loop(1, rows_n, lambda s, c: (col_copy(s).start(), c)[1], 0)

            @pl.when(a != p)
            def _():
                give_in.start()

    row_ids = lax.broadcasted_iota(jnp.int32, (nt, TILE), 0)
    lane_ids = lax.broadcasted_iota(jnp.int32, (nt, TILE), 1)
    counts = lax.fori_loop(
        0, nt, lambda t, c: jnp.where(row_ids == t, count_ref[t], c), jnp.zeros((nt, TILE), jnp.int32))
    small = jnp.zeros((nt, TILE), jnp.float32)
    for s in range(slots):
        hit = (list_ref[:, s:s + 1] == lane_ids) & (counts > s)
        small = jnp.where(hit, 1.0, small)

    def spread(t, carry):
        one = jnp.sum(jnp.where(lane_ids == t, small, 0.0), axis=1, keepdims=True)
        mask[t] = jnp.broadcast_to(one, (nt, TILE))
        return carry

    lax.fori_loop(0, nt, spread, 0)

    def forward(d):
        for h in range(HALVES):
            low, high = 2 * (zz - d) + p, 2 * (zz + d) + p

            @pl.when(zz - d >= 0)
            def _():
                wait_row(low, h)

                @pl.when(zz < lines - 1)
                def _():
                    up(low, h, rowp.at[low, half(h)]).start()

                sib(low, h, rowp.at[low, half(h)]).start()

            @pl.when(zz + d < lines)
            def _():
                wait_row(high, h)

                @pl.when(zz > 0)
                def _():
                    down(high, h, rowp.at[high, half(h)]).start()

                sib(high, h, rowp.at[high, half(h)]).start()

    def keep_of(tile, column):
        wide = [mask[column * ct + j, pl.ds(tile, 1), :] for j in range(ct)]
        return jnp.concatenate(wide, axis=1)

    def tiles(block, first_tile, column):
        parts = []
        for t in range(block.shape[0] // TILE):
            keep = keep_of(first_tile + t, column)
            parts.append(block[t * TILE:(t + 1) * TILE] * keep.astype(jnp.bfloat16))
        return jnp.concatenate(parts, axis=0)

    def product(slot, lhs):
        left = tiles(lhs, tr * vr, slot)
        right = tiles(colp[pl.ds(pl.multiple_of(slot * cb, cb), cb), :], ct * slot, vc)
        return jnp.dot(left, right, preferred_element_type=jnp.float32)

    def add(slot):
        acc[...] += product(slot, rowp[slot])

    def take(d):
        @pl.when(zz - d >= 0)
        def _():
            add(2 * (zz - d) + p)
            for h in range(HALVES):
                wait_row(2 * (zz - d) + 1 - p, h)
            add(2 * (zz - d) + 1 - p)

        @pl.when(zz + d < lines)
        def _():
            add(2 * (zz + d) + p)
            for h in range(HALVES):
                wait_row(2 * (zz + d) + 1 - p, h)
            add(2 * (zz + d) + 1 - p)

    lax.fori_loop(1, lines - 1, lambda d, c: (forward(d), c)[1], 0)

    def wait_col(s, carry):
        here = colp.at[pl.ds(pl.multiple_of((vr + rows_n - s) % rows_n * rb, rb), rb)]
        pltpu.make_async_copy(here, here, col_recv.at[s]).wait()
        return carry

    lax.fori_loop(1, rows_n, wait_col, 0)
    keep_in.wait()
    own_rows = pl.ds(pl.multiple_of(vr * rb, rb), rb)
    acc[...] = product(vc, colp[own_rows, :])
    for h in range(HALVES):
        wait_row(2 * zz + 1 - p, h)
    add(2 * zz + 1 - p)
    lax.fori_loop(1, lines - 1, lambda d, c: (take(d), c)[1], 0)
    forward(lines - 1)
    take(lines - 1)

    lefts, rights = [], []
    for q in range(tr):
        at = pl.ds(pl.multiple_of(vr * rb + q * TILE, TILE), TILE)
        total = acc[q * TILE:(q + 1) * TILE, :]
        keep = keep_of(tr * vr + q, vc)
        t_prod = colp[at, :].astype(jnp.float32) * keep * total
        t_sum, c_sum = 0.0, 0.0
        for j in range(ct):
            cols = slice(j * TILE, (j + 1) * TILE)
            keep_in_tile = mask[tr * vr + q, pl.ds(ct * vc + j, 1), :]
            t_sum += t_prod[:, cols]
            c_sum += inb[q * TILE:(q + 1) * TILE, cols].astype(jnp.float32) * keep_in_tile * total[:, cols]
        lefts.append(jnp.sum(t_sum.T, axis=0, keepdims=True))
        rights.append(jnp.sum(c_sum.T, axis=0, keepdims=True))
    for e in range(reach):
        dest = (vr + e) % rows_n
        t_out, c_out = jnp.zeros((1, TILE), jnp.float32), jnp.zeros((1, TILE), jnp.float32)
        for q in range(tr):
            mine = owner_ref[tr * vr + q] == dest
            t_out = jnp.where(mine, lefts[q], t_out)
            c_out = jnp.where(mine, rights[q], c_out)
        sendbuf[e, 0:1, :] = t_out
        sendbuf[e, 1:2, :] = c_out

    def result(e, i):
        return pltpu.make_async_remote_copy(
            src_ref=sendbuf.at[e], dst_ref=recvbuf.at[e, vc], send_sem=res_send.at[e, i],
            recv_sem=res_recv, device_id=((vr + e) % rows_n, (me_c + i) % cols_n), device_id_type=MESH)

    def each_result(act, act_here):
        for e in range(reach):
            def one(i, carry, e=e):
                here = ((vr + e) % rows_n == me_r) & (i == 0)
                pl.when(jnp.logical_not(here))(lambda: act(result(e, i)))
                return carry

            lax.fori_loop(0, cols_n, one, 0)
            if act_here:
                @pl.when((vr + e) % rows_n == me_r)
                def _():
                    pltpu.make_async_copy(sendbuf.at[e], recvbuf.at[e, vc], res_recv).start()

    each_result(lambda c: c.start(), True)

    @pl.when(a != p)
    def _():
        for h in range(HALVES):
            swaps[h].wait_send()
        give_in.wait_send()

    lax.fori_loop(1, rows_n, lambda s, c: (col_copy(s).wait_send(), c)[1], 0)

    def drain(d, carry):
        for h in range(HALVES):
            low, high = 2 * (zz - d) + p, 2 * (zz + d) + p

            @pl.when(zz - d >= 0)
            def _():
                @pl.when(zz < lines - 1)
                def _():
                    up(low, h, rowp.at[low, half(h)]).wait_send()

                sib(low, h, rowp.at[low, half(h)]).wait_send()

            @pl.when(zz + d < lines)
            def _():
                @pl.when(zz > 0)
                def _():
                    down(high, h, rowp.at[high, half(h)]).wait_send()

                @pl.when(d > 0)
                def _():
                    sib(high, h, rowp.at[high, half(h)]).wait_send()
        return carry

    lax.fori_loop(0, lines, drain, 0)
    each_result(lambda c: c.wait_send(), False)

    pltpu.make_async_copy(recvbuf, recvbuf, res_recv).wait()
    for e in range(reach):
        group = (me_r + rows_n - e) % rows_n
        place = 0
        for other in range(reach):
            place += ((me_r + rows_n - other) % rows_n < group).astype(jnp.int32)
        both = jnp.sum(recvbuf[e], axis=0)
        trans_ref[pl.ds(place, 1), :] = both[0:1, :]
        cyc_ref[pl.ds(place, 1), :] = both[1:2, :]


def solution(mesh):
    rows_n, cols_n = mesh.shape["row"], mesh.shape["col"]

    def per_device(out_weights, in_weights, tile_list, tile_count, owner):
        rb, cb = out_weights.shape
        nt = tile_list.shape[0]
        tr = rb // TILE
        lines = cols_n // 2
        assert rows_n % 2 == 0 and cols_n % 2 == 0 and tr <= rows_n
        n = rows_n * rb
        block = pltpu.VMEM((rb, cb), out_weights.dtype)
        dma = pltpu.SemaphoreType.DMA
        any_space = pl.BlockSpec(memory_space=pl.ANY)
        vmem = pl.BlockSpec(memory_space=pltpu.VMEM)
        smem = pl.BlockSpec(memory_space=pltpu.SMEM)
        trans, cyc = pl.pallas_call(
            functools.partial(kernel, rows_n, cols_n),
            out_shape=[jax.ShapeDtypeStruct((tr, TILE), jnp.float32)] * 2,
            in_specs=[any_space, any_space, vmem, smem, smem],
            out_specs=[vmem, vmem],
            scratch_shapes=[
                block,
                pltpu.VMEM((n, cb), out_weights.dtype),
                pltpu.VMEM((cols_n, rb, cb), out_weights.dtype),
                block,
                pltpu.VMEM((nt, nt, TILE), jnp.float32),
                pltpu.VMEM((rb, cb), jnp.float32),
                pltpu.VMEM((tr, 2, TILE), jnp.float32),
                pltpu.VMEM((tr, cols_n, 2, TILE), jnp.float32),
                dma, dma,
                dma((HALVES,)), dma((HALVES,)),
                dma((rows_n,)), dma((rows_n,)),
                dma, dma,
                dma((cols_n, HALVES)), dma((cols_n, HALVES)), dma((cols_n, HALVES)), dma((cols_n, HALVES)),
                dma((tr, cols_n)), dma,
            ],
            compiler_params=pltpu.CompilerParams(collective_id=0, has_side_effects=True),
            name="census",
        )(out_weights, in_weights, tile_list, tile_count, owner)
        return trans.reshape(rb), cyc.reshape(rb)

    return jax.shard_map(
        per_device, mesh=mesh,
        in_specs=(P("row", "col"), P("row", "col"), P(), P(), P()),
        out_specs=(P("row"), P("row")), check_vma=False)
```

time: 113 us -> 38.1 us (0.34)
  waiting for transfers between devices: 50.5 us -> 0 us
  Pallas kernels: 0 us -> 35.3 us
  between operations: 21.8 us -> 0.65 us
  blocking collectives: 19.5 us -> 0 us
  other arithmetic: 10.2 us -> 0 us
  local copies, waits for them, and re-layouts: 6.35 us -> 1.89 us
  matrix products: 2.35 us -> 0 us
  starting transfers between devices: 1.99 us -> 0 us
    all_gather x2 -> x0, waiting for transfers between devices: 47.3 us -> none  [the longest x1 30 us: per_device(): lax.all_gather(out_owned, 'col', axis=1, tiled=True)]
    pallas_call x0 -> x1, Pallas kernels: none -> 35.3 us  [per_device(): pl.pallas_call(functools.partial(kernel, rows_n, cols_n), out_shape=[jax....]
    psum x1 -> x0, blocking collectives: 19.5 us -> none  [per_device(): transitive, cyclic = lax.psum((transitive_part, cyclic_part), 'col')]
    gather x5 -> x0, local copies, waits for them, and re-layouts: 4.32 us -> none  [the longest x2 3.06 us: per_device(): out_owned = jnp.take(out_panel, owned_nodes, axis=0)]
    ppermute x3 -> x0, waiting for transfers between devices: 3.09 us -> none  [from_behind(): lax.ppermute(x, axis, [(i, (i + by) % length) for i in range(length)])]
    another operation x1 -> x0, other arithmetic: 2.58 us -> none  [to_owners(): jnp.stack(arrivals, axis=0).reshape(reach * pair_slots, TILE, cols_blk)]
    select_n x5 -> x0, other arithmetic: 2.46 us -> none  [the longest x1 1.67 us: per_device(): out_block = jnp.where(out_keep, out_weights, zero_value)]
    dot_general x1 -> x0, matrix products: 2.35 us -> none  [per_device(): jnp.dot(lax.all_gather(out_owned, 'col', axis=1, tiled=True), out_panel,...]
  transfers between devices with their start and end apart: 5 -> 0, of which waited for: 4 -> 0; matrix products, arithmetic and copies ran while one was open for 8% -> 0% of each run, Pallas kernels for 0% -> 0%
where the time goes in v1:
time: 38.1 us; the launch traced here: 37.9 us
  Pallas kernels  35.3 us (93%)
  local copies, waits for them, and re-layouts  1.89 us (5%)
  between operations  0.65 us (2%)
    pallas_call x1, Pallas kernels, per_device(): pl.pallas_call(functools.partial(kernel, rows_n, cols_n), out_shape=[jax....  35.3 us
    unnamed x6, local copies, waits for them, and re-layouts  1.89 us

profile of v1, /device:TPU:0, one launch (start us, length us, event | category | flops | bytes accessed | tf_op | source)
XLA Modules:
  0.0 37.9 jit_solution(6685444981868284606)
XLA Ops:
  0.6 35.3 %census.1 = (f32[4,128]{1,0:T(4,128)}, f32[4,128]{1,0:T(4,128)}) custom-call(bf16[512,256]{1,0:T(8,128)(2,1)} %out_ref.1, bf16[512,256]{1,0:T(8,128)(2,1)} %in_ref.1, s32[16,12]{1,0:T(8,128)} %list_ref.1, s32[16]{0:T(128)} %count_ref.1, s32[16]{0:T(128)} %owner_ref.1), custom_call_target="tpu_custom_call" | custom-call | tf_op jit(solution)/shard_map/census/pallas_call | solution.py:319
  36.0 0.0 copy-start.1
  36.0 0.7 %copy-done.1 = f32[4,128]{1,0:T(4,128)S(1)} copy-done((f32[4,128]{1,0:T(4,128)S(1)}, f32[4,128]{1,0:T(4,128)}, u32[]{:S(2)}) %copy-start.1) | copy-done | bytes 2072
  36.7 0.0 copy-start
  36.7 0.6 %copy.9 = f32[512]{0:T(512)} copy(f32[512]{0:T(512)S(1)} %bitcast.3) | data formatting | bytes 4096
  37.2 0.1 copy-done
  37.3 0.6 %copy.10 = f32[512]{0:T(512)} copy(f32[512]{0:T(512)S(1)} %bitcast.2) | data formatting | bytes 4096
Async XLA Ops:
  36.0 0.7 %copy-start.1 = (f32[4,128]{1,0:T(4,128)S(1)}, f32[4,128]{1,0:T(4,128)}, u32[]{:S(2)}) copy-start(f32[4,128]{1,0:T(4,128)} %get-tuple-element.4) | copy-start | bytes 6148
  36.7 0.7 %copy-start = (f32[4,128]{1,0:T(4,128)S(1)}, f32[4,128]{1,0:T(4,128)}, u32[]{:S(2)}) copy-start(f32[4,128]{1,0:T(4,128)} %get-tuple-element.5) | copy-start | bytes 6148

commit v2 on v1

v2 whole, which is shorter than its diff:
```python
import functools

import jax
import jax.numpy as jnp
from jax import lax
from jax.experimental import pallas as pl
from jax.experimental.pallas import tpu as pltpu
from jax.sharding import PartitionSpec as P

TILE = 128
HALVES = 2
MESH = pl.DeviceIdType.MESH


def kernel(rows_n, cols_n, out_ref, in_ref, list_ref, count_ref, owner_ref, trans_ref, cyc_ref,
           own, colp, rowp, inb, mask, acc, sendbuf, recvbuf,
           load_sem, x_send, own_send, y_send, relay_send, col_recv, in_send, in_recv,
           up_send, dn_send, sib_send, row_recv, res_send, res_recv):
    rb, cb = out_ref.shape
    tr, ct = rb // TILE, cb // TILE
    nt, slots = list_ref.shape
    lines, ys = cols_n // 2, rows_n // 2
    reach = sendbuf.shape[0]
    hb = rb // HALVES
    me_r, me_c = lax.axis_index("row"), lax.axis_index("col")
    yy, p = me_r // 2, me_r % 2
    zz, a = me_c // 2, me_c % 2
    vr, vc = 2 * yy + a, 2 * zz + p

    def home(r, c):
        return (2 * (r // 2) + c % 2, 2 * (c // 2) + r % 2)

    load = pltpu.make_async_copy(out_ref, own, load_sem)
    load.start()

    barrier = pltpu.get_barrier_semaphore()

    def greet(i, carry):
        there = (me_r + i // 2) % rows_n, 2 * zz + (a + i % 2) % 2
        pl.semaphore_signal(barrier, inc=1, device_id=there, device_id_type=MESH)
        return carry

    above, below = (me_c + 2) % cols_n, (me_c + cols_n - 2) % cols_n
    pl.semaphore_signal(barrier, inc=1, device_id=(me_r, above), device_id_type=MESH)
    pl.semaphore_signal(barrier, inc=1, device_id=(me_r, below), device_id_type=MESH)
    lax.fori_loop(1, rows_n * 2, greet, 0)
    load.wait()
    pl.semaphore_wait(barrier, rows_n * 2 + 1)

    def half(h):
        return pl.ds(h * hb, hb)

    def col_at(group, h):
        return colp.at[pl.ds(pl.multiple_of(group * rb + h * hb, hb), hb)]

    def send(src, dst, send_sem, recv_sem, there):
        return pltpu.make_async_remote_copy(
            src_ref=src, dst_ref=dst, send_sem=send_sem, recv_sem=recv_sem, device_id=there, device_id_type=MESH)

    sibling = (2 * yy + 1 - p, me_c)
    across = (2 * yy + a, 2 * zz + 1 - a)

    def over_x(h):
        return send(own.at[half(h)], col_at(me_r, h), x_send.at[h], col_recv.at[me_r, h], across)

    def to_sibling(h):
        return send(own.at[half(h)], col_at(me_r, h), own_send.at[h], col_recv.at[me_r, h], sibling)

    def keep(h):
        return pltpu.make_async_copy(own.at[half(h)], col_at(me_r, h), col_recv.at[me_r, h])

    def over_y(d, h):
        there = (2 * ((yy + d) % ys) + a, me_c)
        return send(own.at[half(h)], col_at(me_r, h), y_send.at[d, h], col_recv.at[me_r, h], there)

    def relay(group, b, d, h):
        there = (2 * ((yy + d) % ys) + p, me_c)
        return send(col_at(group, h), col_at(group, h), relay_send.at[b, d, h], col_recv.at[group, h], there)

    def wait_col(group, h):
        pltpu.make_async_copy(col_at(group, h), col_at(group, h), col_recv.at[group, h]).wait()

    give_in = send(in_ref, inb, in_send, in_recv, across)
    keep_in = pltpu.make_async_copy(in_ref, inb, in_recv)

    @pl.when(a == p)
    def _():
        for h in range(HALVES):
            keep(h).start()

    @pl.when(a != p)
    def _():
        for h in range(HALVES):
            over_x(h).start()

    def start_y():
        for d in range(1, ys):
            for h in range(HALVES):
                over_y(d, h).start()

    @pl.when(a != p)
    def _():
        start_y()
        for h in range(HALVES):
            to_sibling(h).start()

    def up(slot, h, src):
        return send(src, rowp.at[slot, half(h)], up_send.at[slot, h], row_recv.at[slot, h], (me_r, above))

    def down(slot, h, src):
        return send(src, rowp.at[slot, half(h)], dn_send.at[slot, h], row_recv.at[slot, h], (me_r, below))

    def sib(slot, h, src):
        return send(src, rowp.at[slot, half(h)], sib_send.at[slot, h], row_recv.at[slot, h], sibling)

    def wait_row(slot, h):
        pltpu.make_async_copy(rowp.at[slot, half(h)], rowp.at[slot, half(h)], row_recv.at[slot, h]).wait()

    far = lines // 2

    def low_of(d):
        return 2 * ((zz + lines - d) % lines) + p

    def high_of(d):
        return 2 * ((zz + d) % lines) + p

    def goes_up(d, h):
        return d < far or (d == far and h == 0)

    def goes_down(d, h):
        return d < far or (d == far and h == 1)

    for h in range(HALVES):
        wait_col(vr, h)
        if goes_up(1, h):
            up(vc, h, col_at(vr, h)).start()
        if goes_down(1, h):
            down(vc, h, col_at(vr, h)).start()
        sib(vc, h, col_at(vr, h)).start()

    @pl.when(a == p)
    def _():
        start_y()

    @pl.when(a != p)
    def _():
        give_in.start()
        for d in range(1, ys):
            for h in range(HALVES):
                relay(vr, 0, d, h).start()

    @pl.when(a == p)
    def _():
        keep_in.start()

    row_ids = lax.broadcasted_iota(jnp.int32, (nt, TILE), 0)
    lane_ids = lax.broadcasted_iota(jnp.int32, (nt, TILE), 1)
    counts = lax.fori_loop(
        0, nt, lambda t, c: jnp.where(row_ids == t, count_ref[t], c), jnp.zeros((nt, TILE), jnp.int32))
    small = jnp.zeros((nt, TILE), jnp.float32)
    for s in range(slots):
        hit = (list_ref[:, s:s + 1] == lane_ids) & (counts > s)
        small = jnp.where(hit, 1.0, small)

    def spread(t, carry):
        one = jnp.sum(jnp.where(lane_ids == t, small, 0.0), axis=1, keepdims=True)
        mask[t] = jnp.broadcast_to(one, (nt, TILE))
        return carry

    lax.fori_loop(0, nt, spread, 0)

    def forward(d):
        for h in range(HALVES):
            if goes_up(d, h):
                slot = low_of(d)
                wait_row(slot, h)
                if goes_up(d + 1, h):
                    up(slot, h, rowp.at[slot, half(h)]).start()
                sib(slot, h, rowp.at[slot, half(h)]).start()
            if goes_down(d, h):
                slot = high_of(d)
                wait_row(slot, h)
                if goes_down(d + 1, h):
                    down(slot, h, rowp.at[slot, half(h)]).start()
                sib(slot, h, rowp.at[slot, half(h)]).start()
            if d == 1 and h == 0:
                @pl.when(a == p)
                def _():
                    for k in range(HALVES):
                        over_x(k).start()

    def keep_of(tile, column):
        wide = [mask[column * ct + j, pl.ds(tile, 1), :] for j in range(ct)]
        return jnp.concatenate(wide, axis=1)

    def tiles(block, first_tile, column):
        parts = []
        for t in range(block.shape[0] // TILE):
            keep = keep_of(first_tile + t, column)
            parts.append(block[t * TILE:(t + 1) * TILE] * keep.astype(jnp.bfloat16))
        return jnp.concatenate(parts, axis=0)

    def product(slot, lhs):
        left = tiles(lhs, tr * vr, slot)
        right = tiles(colp[pl.ds(pl.multiple_of(slot * cb, cb), cb), :], ct * slot, vc)
        return jnp.dot(left, right, preferred_element_type=jnp.float32)

    def add(slot):
        acc[...] += product(slot, rowp[slot])

    def take(slot):
        add(slot)
        for h in range(HALVES):
            wait_row(slot + 1 - 2 * p, h)
        add(slot + 1 - 2 * p)

    other = 2 * yy + 1 - a
    forward(1)

    @pl.when(a != p)
    def _():
        for h in range(HALVES):
            wait_col(other, h)
            for d in range(1, ys):
                relay(other, 1, d, h).start()

    @pl.when(a == p)
    def _():
        for h in range(HALVES):
            wait_col(other, h)

    for d in range(2, far):
        forward(d)

    def wait_cols(i, carry):
        for h in range(HALVES):
            wait_col((2 * yy + i) % rows_n, h)
        return carry

    if far > 1:
        forward(far)
    lax.fori_loop(2, rows_n, wait_cols, 0)
    acc[...] = product(vc, colp[pl.ds(pl.multiple_of(vr * rb, rb), rb), :])
    for h in range(HALVES):
        wait_row(vc + 1 - 2 * p, h)
    add(vc + 1 - 2 * p)

    def take_both(d, carry):
        take(low_of(d))
        take(high_of(d))
        return carry

    lax.fori_loop(1, far, take_both, 0)
    take(low_of(far))
    keep_in.wait()

    lefts, rights = [], []
    for q in range(tr):
        at = pl.ds(pl.multiple_of(vr * rb + q * TILE, TILE), TILE)
        total = acc[q * TILE:(q + 1) * TILE, :]
        keep = keep_of(tr * vr + q, vc)
        t_prod = colp[at, :].astype(jnp.float32) * keep * total
        t_sum, c_sum = 0.0, 0.0
        for j in range(ct):
            cols = slice(j * TILE, (j + 1) * TILE)
            keep_in_tile = mask[tr * vr + q, pl.ds(ct * vc + j, 1), :]
            t_sum += t_prod[:, cols]
            c_sum += inb[q * TILE:(q + 1) * TILE, cols].astype(jnp.float32) * keep_in_tile * total[:, cols]
        lefts.append(jnp.sum(t_sum.T, axis=0, keepdims=True))
        rights.append(jnp.sum(c_sum.T, axis=0, keepdims=True))
    for e in range(reach):
        dest = (vr + e) % rows_n
        t_out, c_out = jnp.zeros((1, TILE), jnp.float32), jnp.zeros((1, TILE), jnp.float32)
        for q in range(tr):
            mine = owner_ref[tr * vr + q] == dest
            t_out = jnp.where(mine, lefts[q], t_out)
            c_out = jnp.where(mine, rights[q], c_out)
        sendbuf[e, 0:1, :] = t_out
        sendbuf[e, 1:2, :] = c_out

    def result(e, i):
        return pltpu.make_async_remote_copy(
            src_ref=sendbuf.at[e], dst_ref=recvbuf.at[e, vc], send_sem=res_send.at[e, i],
            recv_sem=res_recv, device_id=((vr + e) % rows_n, (me_c + i) % cols_n), device_id_type=MESH)

    def each_result(act, act_here):
        for e in range(reach):
            def one(i, carry, e=e):
                here = ((vr + e) % rows_n == me_r) & (i == 0)
                pl.when(jnp.logical_not(here))(lambda: act(result(e, i)))
                return carry

            lax.fori_loop(0, cols_n, one, 0)
            if act_here:
                @pl.when((vr + e) % rows_n == me_r)
                def _():
                    pltpu.make_async_copy(sendbuf.at[e], recvbuf.at[e, vc], res_recv).start()

    each_result(lambda c: c.start(), True)

    @pl.when(a != p)
    def _():
        give_in.wait_send()
        for h in range(HALVES):
            to_sibling(h).wait_send()
            for d in range(1, ys):
                relay(vr, 0, d, h).wait_send()
                relay(other, 1, d, h).wait_send()

    for h in range(HALVES):
        over_x(h).wait_send()
        for d in range(1, ys):
            over_y(d, h).wait_send()

    for d in range(far + 1):
        for h in range(HALVES):
            low, high = low_of(d), high_of(d)
            if goes_up(d, h):
                if goes_up(d + 1, h):
                    up(low, h, rowp.at[low, half(h)]).wait_send()
                sib(low, h, rowp.at[low, half(h)]).wait_send()
            if goes_down(d, h):
                if goes_down(d + 1, h):
                    down(high, h, rowp.at[high, half(h)]).wait_send()
                if d > 0:
                    sib(high, h, rowp.at[high, half(h)]).wait_send()
    each_result(lambda c: c.wait_send(), False)

    pltpu.make_async_copy(recvbuf, recvbuf, res_recv).wait()
    for e in range(reach):
        group = (me_r + rows_n - e) % rows_n
        place = 0
        for other in range(reach):
            place += ((me_r + rows_n - other) % rows_n < group).astype(jnp.int32)
        both = jnp.sum(recvbuf[e], axis=0)
        at = pl.ds(pl.multiple_of(place * TILE, TILE), TILE)
        trans_ref[at] = both[0]
        cyc_ref[at] = both[1]


def solution(mesh):
    rows_n, cols_n = mesh.shape["row"], mesh.shape["col"]

    def per_device(out_weights, in_weights, tile_list, tile_count, owner):
        rb, cb = out_weights.shape
        nt = tile_list.shape[0]
        tr = rb // TILE
        lines = cols_n // 2
        assert rows_n % 2 == 0 and lines % 2 == 0 and lines > 2 and tr <= rows_n
        n = rows_n * rb
        block = pltpu.VMEM((rb, cb), out_weights.dtype)
        dma = pltpu.SemaphoreType.DMA
        any_space = pl.BlockSpec(memory_space=pl.ANY)
        vmem = pl.BlockSpec(memory_space=pltpu.VMEM)
        smem = pl.BlockSpec(memory_space=pltpu.SMEM)
        trans, cyc = pl.pallas_call(
            functools.partial(kernel, rows_n, cols_n),
            out_shape=[jax.ShapeDtypeStruct((rb,), jnp.float32)] * 2,
            in_specs=[any_space, any_space, vmem, smem, smem],
            out_specs=[vmem, vmem],
            scratch_shapes=[
                block,
                pltpu.VMEM((n, cb), out_weights.dtype),
                pltpu.VMEM((cols_n, rb, cb), out_weights.dtype),
                block,
                pltpu.VMEM((nt, nt, TILE), jnp.float32),
                pltpu.VMEM((rb, cb), jnp.float32),
                pltpu.VMEM((tr, 2, TILE), jnp.float32),
                pltpu.VMEM((tr, cols_n, 2, TILE), jnp.float32),
                dma, dma((HALVES,)), dma((HALVES,)),
                dma((rows_n // 2, HALVES)), dma((2, rows_n // 2, HALVES)), dma((rows_n, HALVES)),
                dma, dma,
                dma((cols_n, HALVES)), dma((cols_n, HALVES)), dma((cols_n, HALVES)), dma((cols_n, HALVES)),
                dma((tr, cols_n)), dma,
            ],
            compiler_params=pltpu.CompilerParams(collective_id=0, has_side_effects=True),
            name="census",
        )(out_weights, in_weights, tile_list, tile_count, owner)
        return trans, cyc

    return jax.shard_map(
        per_device, mesh=mesh,
        in_specs=(P("row", "col"), P("row", "col"), P(), P(), P()),
        out_specs=(P("row"), P("row")), check_vma=False)
```

time: 38.1 us -> 39.5 us (1.037)
  Pallas kernels: 35.3 us -> 36.7 us
    pallas_call x1, Pallas kernels: 35.3 us -> 36.7 us  [per_device(): pl.pallas_call(functools.partial(kernel, rows_n, cols_n), out_shape=[jax....]
where the time goes in v2:
time: 39.5 us; the launch traced here: 39.3 us
  Pallas kernels  36.7 us (93%)
  local copies, waits for them, and re-layouts  1.89 us (5%)
  between operations  0.65 us (2%)
    pallas_call x1, Pallas kernels, per_device(): pl.pallas_call(functools.partial(kernel, rows_n, cols_n), out_shape=[jax....  36.7 us
    unnamed x6, local copies, waits for them, and re-layouts  1.89 us

profile of v2, /device:TPU:0, one launch (start us, length us, event | category | flops | bytes accessed | tf_op | source)
XLA Modules:
  0.0 39.3 jit_solution(32004373508410363)
XLA Ops:
  0.6 36.7 %census.1 = (f32[512]{0:T(512)}, f32[512]{0:T(512)}) custom-call(bf16[512,256]{1,0:T(8,128)(2,1)} %out_ref.1, bf16[512,256]{1,0:T(8,128)(2,1)} %in_ref.1, s32[16,12]{1,0:T(8,128)} %list_ref.1, s32[16]{0:T(128)} %count_ref.1, s32[16]{0:T(128)} %owner_ref.1), custom_call_target="tpu_custom_call" | custom-call | tf_op jit(solution)/shard_map/census/pallas_call | solution.py:356
  37.4 0.0 copy-start.1
  37.4 0.7 %copy-done.1 = f32[512]{0:T(512)S(1)} copy-done((f32[512]{0:T(512)S(1)}, f32[512]{0:T(512)}, u32[]{:S(2)}) %copy-start.1) | copy-done | bytes 2072
  38.1 0.0 copy-start
  38.1 0.6 %copy.9 = f32[512]{0:T(512)} copy(f32[512]{0:T(512)S(1)} %copy-done.1) | data formatting | bytes 4096
  38.6 0.1 copy-done
  38.7 0.6 %copy.10 = f32[512]{0:T(512)} copy(f32[512]{0:T(512)S(1)} %copy-done) | data formatting | bytes 4096
Async XLA Ops:
  37.4 0.7 %copy-start.1 = (f32[512]{0:T(512)S(1)}, f32[512]{0:T(512)}, u32[]{:S(2)}) copy-start(f32[512]{0:T(512)} %get-tuple-element.4) | copy-start | bytes 6148
  38.1 0.7 %copy-start = (f32[512]{0:T(512)S(1)}, f32[512]{0:T(512)}, u32[]{:S(2)}) copy-start(f32[512]{0:T(512)} %get-tuple-element.5) | copy-start | bytes 6148

commit v3 on v2

--- a/solution.py
+++ b/solution.py
@@ -40,12 +40,21 @@
         pl.semaphore_signal(barrier, inc=1, device_id=there, device_id_type=MESH)
         return carry
 
-    above, below = (me_c + 2) % cols_n, (me_c + cols_n - 2) % cols_n
-    pl.semaphore_signal(barrier, inc=1, device_id=(me_r, above), device_id_type=MESH)
-    pl.semaphore_signal(barrier, inc=1, device_id=(me_r, below), device_id_type=MESH)
+    above, below = me_c + 2, me_c - 2
+    has_above, has_below = zz < lines - 1, zz > 0
+
+    @pl.when(has_above)
+    def _():
+        pl.semaphore_signal(barrier, inc=1, device_id=(me_r, above), device_id_type=MESH)
+
+    @pl.when(has_below)
+    def _():
+        pl.semaphore_signal(barrier, inc=1, device_id=(me_r, below), device_id_type=MESH)
+
     lax.fori_loop(1, rows_n * 2, greet, 0)
     load.wait()
-    pl.semaphore_wait(barrier, rows_n * 2 + 1)
+    expected = rows_n * 2 - 1 + has_above.astype(jnp.int32) + has_below.astype(jnp.int32)
+    pl.semaphore_wait(barrier, expected)
 
     def half(h):
         return pl.ds(h * hb, hb)
@@ -116,26 +125,10 @@
     def wait_row(slot, h):
         pltpu.make_async_copy(rowp.at[slot, half(h)], rowp.at[slot, half(h)], row_recv.at[slot, h]).wait()
 
-    far = lines // 2
-
-    def low_of(d):
-        return 2 * ((zz + lines - d) % lines) + p
-
-    def high_of(d):
-        return 2 * ((zz + d) % lines) + p
-
-    def goes_up(d, h):
-        return d < far or (d == far and h == 0)
-
-    def goes_down(d, h):
-        return d < far or (d == far and h == 1)
-
     for h in range(HALVES):
         wait_col(vr, h)
-        if goes_up(1, h):
-            up(vc, h, col_at(vr, h)).start()
-        if goes_down(1, h):
-            down(vc, h, col_at(vr, h)).start()
+        pl.when(has_above)(lambda h=h: up(vc, h, col_at(vr, h)).start())
+        pl.when(has_below)(lambda h=h: down(vc, h, col_at(vr, h)).start())
         sib(vc, h, col_at(vr, h)).start()
 
     @pl.when(a == p)
@@ -169,25 +162,27 @@
 
     lax.fori_loop(0, nt, spread, 0)
 
+    def low_of(d):
+        return 2 * (zz - d) + p
+
+    def high_of(d):
+        return 2 * (zz + d) + p
+
     def forward(d):
         for h in range(HALVES):
-            if goes_up(d, h):
+            @pl.when(zz - d >= 0)
+            def _():
                 slot = low_of(d)
                 wait_row(slot, h)
-                if goes_up(d + 1, h):
-                    up(slot, h, rowp.at[slot, half(h)]).start()
+                pl.when(has_above)(lambda: up(slot, h, rowp.at[slot, half(h)]).start())
                 sib(slot, h, rowp.at[slot, half(h)]).start()
-            if goes_down(d, h):
+
+            @pl.when(zz + d < lines)
+            def _():
                 slot = high_of(d)
                 wait_row(slot, h)
-                if goes_down(d + 1, h):
-                    down(slot, h, rowp.at[slot, half(h)]).start()
+                pl.when(has_below)(lambda: down(slot, h, rowp.at[slot, half(h)]).start())
                 sib(slot, h, rowp.at[slot, half(h)]).start()
-            if d == 1 and h == 0:
-                @pl.when(a == p)
-                def _():
-                    for k in range(HALVES):
-                        over_x(k).start()
 
     def keep_of(tile, column):
         wide = [mask[column * ct + j, pl.ds(tile, 1), :] for j in range(ct)]
@@ -217,6 +212,11 @@
     other = 2 * yy + 1 - a
     forward(1)
 
+    @pl.when(a == p)
+    def _():
+        for h in range(HALVES):
+            over_x(h).start()
+
     @pl.when(a != p)
     def _():
         for h in range(HALVES):
@@ -229,30 +229,27 @@
         for h in range(HALVES):
             wait_col(other, h)
 
-    for d in range(2, far):
-        forward(d)
+    lax.fori_loop(2, lines - 1, lambda d, c: (forward(d), c)[1], 0)
 
     def wait_cols(i, carry):
         for h in range(HALVES):
             wait_col((2 * yy + i) % rows_n, h)
         return carry
 
-    if far > 1:
-        forward(far)
     lax.fori_loop(2, rows_n, wait_cols, 0)
     acc[...] = product(vc, colp[pl.ds(pl.multiple_of(vr * rb, rb), rb), :])
     for h in range(HALVES):
         wait_row(vc + 1 - 2 * p, h)
     add(vc + 1 - 2 * p)
 
-    def take_both(d, carry):
-        take(low_of(d))
-        take(high_of(d))
-        return carry
-
-    lax.fori_loop(1, far, take_both, 0)
-    take(low_of(far))
+    def take_both(d):
+        pl.when(zz - d >= 0)(lambda: take(low_of(d)))
+        pl.when(zz + d < lines)(lambda: take(high_of(d)))
+
+    lax.fori_loop(1, lines - 1, lambda d, c: (take_both(d), c)[1], 0)
     keep_in.wait()
+    forward(lines - 1)
+    take_both(lines - 1)
 
     lefts, rights = [], []
     for q in range(tr):
@@ -312,18 +309,22 @@
         for d in range(1, ys):
             over_y(d, h).wait_send()
 
-    for d in range(far + 1):
+    def drain(d, carry):
         for h in range(HALVES):
             low, high = low_of(d), high_of(d)
-            if goes_up(d, h):
-                if goes_up(d + 1, h):
-                    up(low, h, rowp.at[low, half(h)]).wait_send()
+
+            @pl.when(zz - d >= 0)
+            def _():
+                pl.when(has_above)(lambda: up(low, h, rowp.at[low, half(h)]).wait_send())
                 sib(low, h, rowp.at[low, half(h)]).wait_send()
-            if goes_down(d, h):
-                if goes_down(d + 1, h):
-                    down(high, h, rowp.at[high, half(h)]).wait_send()
-                if d > 0:
-                    sib(high, h, rowp.at[high, half(h)]).wait_send()
+
+            @pl.when(zz + d < lines)
+            def _():
+                pl.when(has_below)(lambda: down(high, h, rowp.at[high, half(h)]).wait_send())
+                pl.when(d > 0)(lambda: sib(high, h, rowp.at[high, half(h)]).wait_send())
+        return carry
+
+    lax.fori_loop(0, lines, drain, 0)
     each_result(lambda c: c.wait_send(), False)
 
     pltpu.make_async_copy(recvbuf, recvbuf, res_recv).wait()
@@ -346,7 +347,7 @@
         nt = tile_list.shape[0]
         tr = rb // TILE
         lines = cols_n // 2
-        assert rows_n % 2 == 0 and lines % 2 == 0 and lines > 2 and tr <= rows_n
+        assert rows_n % 2 == 0 and cols_n % 2 == 0 and tr <= rows_n
         n = rows_n * rb
         block = pltpu.VMEM((rb, cb), out_weights.dtype)
         dma = pltpu.SemaphoreType.DMA
@@ -376,7 +377,13 @@
             compiler_params=pltpu.CompilerParams(collective_id=0, has_side_effects=True),
             name="census",
         )(out_weights, in_weights, tile_list, tile_count, owner)
-        return trans, cyc
+        def last(t_in, c_in, t_out, c_out):
+            t_out[...] = t_in[...]
+            c_out[...] = c_in[...]
+
+        return pl.pallas_call(
+            last, out_shape=[jax.ShapeDtypeStruct((rb,), jnp.float32)] * 2,
+            in_specs=[vmem, vmem], out_specs=[vmem, vmem], name="last")(trans, cyc)
 
     return jax.shard_map(
         per_device, mesh=mesh,

time: 39.5 us -> 35.4 us (0.90)
  Pallas kernels: 36.7 us -> 34.5 us
  local copies, waits for them, and re-layouts: 1.89 us -> 0 us
    pallas_call x1, Pallas kernels: 36.7 us -> 33.3 us  [per_device(): pl.pallas_call(functools.partial(kernel, rows_n, cols_n), out_shape=[jax....]
    unnamed x6 -> x0, local copies, waits for them, and re-layouts: 1.89 us -> none
    pallas_call x0 -> x1, Pallas kernels: none -> 1.26 us  [per_device(): pl.pallas_call(last, out_shape=[jax.ShapeDtypeStruct((rb,), jnp.float32)]...]
where the time goes in v3:
time: 35.4 us; the launch traced here: 35.2 us
  Pallas kernels  34.5 us (97%)
  between operations  0.64 us (2%)
    pallas_call x1, Pallas kernels, per_device(): pl.pallas_call(functools.partial(kernel, rows_n, cols_n), out_shape=[jax....  33.3 us
    pallas_call x1, Pallas kernels, per_device(): pl.pallas_call(last, out_shape=[jax.ShapeDtypeStruct((rb,), jnp.float32)]...  1.26 us

profile of v3, /device:TPU:0, one launch (start us, length us, event | category | flops | bytes accessed | tf_op | source)
XLA Modules:
  0.0 35.2 jit_solution(3080996979912174049)
XLA Ops:
  0.6 33.3 %census.1 = (f32[512]{0:T(512)}, f32[512]{0:T(512)}) custom-call(bf16[512,256]{1,0:T(8,128)(2,1)} %out_ref.1, bf16[512,256]{1,0:T(8,128)(2,1)} %in_ref.1, s32[16,12]{1,0:T(8,128)} %list_ref.1, s32[16]{0:T(128)} %count_ref.1, s32[16]{0:T(128)} %owner_ref.1), custom_call_target="tpu_custom_call" | custom-call | tf_op jit(solution)/shard_map/census/pallas_call | solution.py:357
  33.9 1.3 %last.1 = (f32[512]{0:T(512)}, f32[512]{0:T(512)}) custom-call(f32[512]{0:T(512)} %get-tuple-element.4.t_in, f32[512]{0:T(512)} %get-tuple-element.5.c_in), custom_call_target="tpu_custom_call" | custom-call | tf_op jit(solution)/shard_map/last/pallas_call | solution.py:384

commit v4 on v3

--- a/solution.py
+++ b/solution.py
@@ -52,100 +52,6 @@
         pl.semaphore_signal(barrier, inc=1, device_id=(me_r, below), device_id_type=MESH)
 
     lax.fori_loop(1, rows_n * 2, greet, 0)
-    load.wait()
-    expected = rows_n * 2 - 1 + has_above.astype(jnp.int32) + has_below.astype(jnp.int32)
-    pl.semaphore_wait(barrier, expected)
-
-    def half(h):
-        return pl.ds(h * hb, hb)
-
-    def col_at(group, h):
-        return colp.at[pl.ds(pl.multiple_of(group * rb + h * hb, hb), hb)]
-
-    def send(src, dst, send_sem, recv_sem, there):
-        return pltpu.make_async_remote_copy(
-            src_ref=src, dst_ref=dst, send_sem=send_sem, recv_sem=recv_sem, device_id=there, device_id_type=MESH)
-
-    sibling = (2 * yy + 1 - p, me_c)
-    across = (2 * yy + a, 2 * zz + 1 - a)
-
-    def over_x(h):
-        return send(own.at[half(h)], col_at(me_r, h), x_send.at[h], col_recv.at[me_r, h], across)
-
-    def to_sibling(h):
-        return send(own.at[half(h)], col_at(me_r, h), own_send.at[h], col_recv.at[me_r, h], sibling)
-
-    def keep(h):
-        return pltpu.make_async_copy(own.at[half(h)], col_at(me_r, h), col_recv.at[me_r, h])
-
-    def over_y(d, h):
-        there = (2 * ((yy + d) % ys) + a, me_c)
-        return send(own.at[half(h)], col_at(me_r, h), y_send.at[d, h], col_recv.at[me_r, h], there)
-
-    def relay(group, b, d, h):
-        there = (2 * ((yy + d) % ys) + p, me_c)
-        return send(col_at(group, h), col_at(group, h), relay_send.at[b, d, h], col_recv.at[group, h], there)
-
-    def wait_col(group, h):
-        pltpu.make_async_copy(col_at(group, h), col_at(group, h), col_recv.at[group, h]).wait()
-
-    give_in = send(in_ref, inb, in_send, in_recv, across)
-    keep_in = pltpu.make_async_copy(in_ref, inb, in_recv)
-
-    @pl.when(a == p)
-    def _():
-        for h in range(HALVES):
-            keep(h).start()
-
-    @pl.when(a != p)
-    def _():
-        for h in range(HALVES):
-            over_x(h).start()
-
-    def start_y():
-        for d in range(1, ys):
-            for h in range(HALVES):
-                over_y(d, h).start()
-
-    @pl.when(a != p)
-    def _():
-        start_y()
-        for h in range(HALVES):
-            to_sibling(h).start()
-
-    def up(slot, h, src):
-        return send(src, rowp.at[slot, half(h)], up_send.at[slot, h], row_recv.at[slot, h], (me_r, above))
-
-    def down(slot, h, src):
-        return send(src, rowp.at[slot, half(h)], dn_send.at[slot, h], row_recv.at[slot, h], (me_r, below))
-
-    def sib(slot, h, src):
-        return send(src, rowp.at[slot, half(h)], sib_send.at[slot, h], row_recv.at[slot, h], sibling)
-
-    def wait_row(slot, h):
-        pltpu.make_async_copy(rowp.at[slot, half(h)], rowp.at[slot, half(h)], row_recv.at[slot, h]).wait()
-
-    for h in range(HALVES):
-        wait_col(vr, h)
-        pl.when(has_above)(lambda h=h: up(vc, h, col_at(vr, h)).start())
-        pl.when(has_below)(lambda h=h: down(vc, h, col_at(vr, h)).start())
-        sib(vc, h, col_at(vr, h)).start()
-
-    @pl.when(a == p)
-    def _():
-        start_y()
-
-    @pl.when(a != p)
-    def _():
-        give_in.start()
-        for d in range(1, ys):
-            for h in range(HALVES):
-                relay(vr, 0, d, h).start()
-
-    @pl.when(a == p)
-    def _():
-        keep_in.start()
-
     row_ids = lax.broadcasted_iota(jnp.int32, (nt, TILE), 0)
     lane_ids = lax.broadcasted_iota(jnp.int32, (nt, TILE), 1)
     counts = lax.fori_loop(
@@ -161,6 +67,100 @@
         return carry
 
     lax.fori_loop(0, nt, spread, 0)
+
+    load.wait()
+    expected = rows_n * 2 - 1 + has_above.astype(jnp.int32) + has_below.astype(jnp.int32)
+    pl.semaphore_wait(barrier, expected)
+
+    def half(h):
+        return pl.ds(h * hb, hb)
+
+    def col_at(group, h):
+        return colp.at[pl.ds(pl.multiple_of(group * rb + h * hb, hb), hb)]
+
+    def send(src, dst, send_sem, recv_sem, there):
+        return pltpu.make_async_remote_copy(
+            src_ref=src, dst_ref=dst, send_sem=send_sem, recv_sem=recv_sem, device_id=there, device_id_type=MESH)
+
+    sibling = (2 * yy + 1 - p, me_c)
+    across = (2 * yy + a, 2 * zz + 1 - a)
+
+    def over_x(h):
+        return send(own.at[half(h)], col_at(me_r, h), x_send.at[h], col_recv.at[me_r, h], across)
+
+    def to_sibling(h):
+        return send(own.at[half(h)], col_at(me_r, h), own_send.at[h], col_recv.at[me_r, h], sibling)
+
+    def keep(h):
+        return pltpu.make_async_copy(own.at[half(h)], col_at(me_r, h), col_recv.at[me_r, h])
+
+    def over_y(d, h):
+        there = (2 * ((yy + d) % ys) + a, me_c)
+        return send(own.at[half(h)], col_at(me_r, h), y_send.at[d, h], col_recv.at[me_r, h], there)
+
+    def relay(group, b, d, h):
+        there = (2 * ((yy + d) % ys) + p, me_c)
+        return send(col_at(group, h), col_at(group, h), relay_send.at[b, d, h], col_recv.at[group, h], there)
+
+    def wait_col(group, h):
+        pltpu.make_async_copy(col_at(group, h), col_at(group, h), col_recv.at[group, h]).wait()
+
+    give_in = send(in_ref, inb, in_send, in_recv, across)
+    keep_in = pltpu.make_async_copy(in_ref, inb, in_recv)
+
+    @pl.when(a == p)
+    def _():
+        for h in range(HALVES):
+            keep(h).start()
+
+    @pl.when(a != p)
+    def _():
+        for h in range(HALVES):
+            over_x(h).start()
+
+    def start_y():
+        for d in range(1, ys):
+            for h in range(HALVES):
+                over_y(d, h).start()
+
+    @pl.when(a != p)
+    def _():
+        start_y()
+        for h in range(HALVES):
+            to_sibling(h).start()
+
+    def up(slot, h, src):
+        return send(src, rowp.at[slot, half(h)], up_send.at[slot, h], row_recv.at[slot, h], (me_r, above))
+
+    def down(slot, h, src):
+        return send(src, rowp.at[slot, half(h)], dn_send.at[slot, h], row_recv.at[slot, h], (me_r, below))
+
+    def sib(slot, h, src):
+        return send(src, rowp.at[slot, half(h)], sib_send.at[slot, h], row_recv.at[slot, h], sibling)
+
+    def wait_row(slot, h):
+        pltpu.make_async_copy(rowp.at[slot, half(h)], rowp.at[slot, half(h)], row_recv.at[slot, h]).wait()
+
+    for h in range(HALVES):
+        wait_col(vr, h)
+        pl.when(has_above)(lambda h=h: up(vc, h, col_at(vr, h)).start())
+        pl.when(has_below)(lambda h=h: down(vc, h, col_at(vr, h)).start())
+        sib(vc, h, col_at(vr, h)).start()
+
+    @pl.when(a == p)
+    def _():
+        start_y()
+
+    @pl.when(a != p)
+    def _():
+        give_in.start()
+        for d in range(1, ys):
+            for h in range(HALVES):
+                relay(vr, 0, d, h).start()
+
+    @pl.when(a == p)
+    def _():
+        keep_in.start()
 
     def low_of(d):
         return 2 * (zz - d) + p

time: 35.4 us -> 35.5 us (level)
  no operation moved by 1% of the time
where the time goes in v4:
time: 35.5 us; the launch traced here: 35.3 us
  Pallas kernels  34.6 us (97%)
  between operations  0.64 us (2%)
    pallas_call x1, Pallas kernels, per_device(): pl.pallas_call(functools.partial(kernel, rows_n, cols_n), out_shape=[jax....  33.4 us
    pallas_call x1, Pallas kernels, per_device(): pl.pallas_call(last, out_shape=[jax.ShapeDtypeStruct((rb,), jnp.float32)]...  1.26 us

profile of v4, /device:TPU:0, one launch (start us, length us, event | category | flops | bytes accessed | tf_op | source)
XLA Modules:
  0.0 35.3 jit_solution(6093980154564709982)
XLA Ops:
  0.6 33.4 %census.1 = (f32[512]{0:T(512)}, f32[512]{0:T(512)}) custom-call(bf16[512,256]{1,0:T(8,128)(2,1)} %out_ref.1, bf16[512,256]{1,0:T(8,128)(2,1)} %in_ref.1, s32[16,12]{1,0:T(8,128)} %list_ref.1, s32[16]{0:T(128)} %count_ref.1, s32[16]{0:T(128)} %owner_ref.1), custom_call_target="tpu_custom_call" | custom-call | tf_op jit(solution)/shard_map/census/pallas_call | solution.py:357
  34.0 1.3 %last.1 = (f32[512]{0:T(512)}, f32[512]{0:T(512)}) custom-call(f32[512]{0:T(512)} %get-tuple-element.4.t_in, f32[512]{0:T(512)} %get-tuple-element.5.c_in), custom_call_target="tpu_custom_call" | custom-call | tf_op jit(solution)/shard_map/last/pallas_call | solution.py:384
